TPU v7x, 8 devices: a whole 2x2x1 slice. The times are simulated.
8 devices in a mesh: right: 2 (over z, y), left: 4 (over x, core).
Axes of the slice: x: 2, y: 2, z: 1, core: 2. Of those that a mesh axis runs over, the one named last changes fastest.
Arguments:
- psi_init: float32 [2048, 2, 2, 2048], P('left', None, None, 'right')
- env_left: float32 [2048, 3, 2048], P('left')
- env_right: float32 [2048, 3, 2048], P('right')
- mpo_pair: float32 [3, 3, 2, 2, 2, 2], replicated
Outputs:
- output 1: float32 [5], replicated
- output 2: float32 [5], replicated
- output 3: float32 [2048, 2, 2, 2048], P('left', None, None, 'right')
All inputs are finite; a program needn't handle non-finite values.
Results may differ from a plain program's by a relative error of at most 0.001.
Values sent between devices are 32-bit elements.
A program may use at most 1 GiB of HBM per device.

v0:
```python
import math
import jax
import jax.numpy as jnp
from jax import lax
from jax.sharding import PartitionSpec as P

KRYLOV_STEPS = 5
PREC_MODE = lax.Precision.HIGHEST
BOTH_AXES = ("right", "left")


def project_out(krylov_basis, residual, coeffs):
    for vec_idx, basis_vec in enumerate(krylov_basis):
        residual = residual - coeffs[vec_idx] * basis_vec
    return residual


def global_dots(krylov_basis, residual):
    local_dots = jnp.stack([jnp.sum(basis_vec * residual) for basis_vec in krylov_basis])
    return lax.psum(local_dots, BOTH_AXES)


def solution(mesh):
    n_devices = mesh.shape["left"] * mesh.shape["right"]
    psi_spec = P("left", None, None, "right")

    def local_fn(psi_loc, env_left, env_right, mpo_pair):
        left_full = lax.all_to_all(env_left, "left", 2, 0, tiled=True)

        def apply_ham(in_vec):
            vec_full = lax.all_gather(in_vec, "left", axis=0, tiled=True)
            stage_one = jnp.einsum("alc,asub->lcsub", left_full, vec_full, precision=PREC_MODE, preferred_element_type=jnp.float32)
            stage_two = jnp.einsum("lrsutv,lcsub->rtvcb", mpo_pair, stage_one, precision=PREC_MODE, preferred_element_type=jnp.float32)
            part_out = jnp.einsum("rtvcb,bre->tvce", stage_two, env_right, precision=PREC_MODE, preferred_element_type=jnp.float32)
            reduced = lax.psum_scatter(part_out, "right", scatter_dimension=3, tiled=True)
            return jnp.transpose(reduced, (2, 0, 1, 3))

        init_norm = jnp.sqrt(lax.psum(jnp.sum(psi_loc * psi_loc), BOTH_AXES))
        krylov_basis = [psi_loc / init_norm]
        alpha_list = []
        beta_list = []
        for step_idx in range(KRYLOV_STEPS):
            residual = apply_ham(krylov_basis[-1])
            first_pass = global_dots(krylov_basis, residual)
            alpha_list.append(first_pass[-1])
            residual = project_out(krylov_basis, residual, first_pass)
            second_pass = global_dots(krylov_basis, residual)
            residual = project_out(krylov_basis, residual, second_pass)
            beta_val = jnp.sqrt(lax.psum(jnp.sum(residual * residual), BOTH_AXES))
            beta_list.append(beta_val)
            krylov_basis.append(residual / beta_val)
        out_scale = math.sqrt(float(psi_loc.size * n_devices))
        return jnp.stack(alpha_list), jnp.stack(beta_list), krylov_basis[-1] * out_scale

    lanczos_run = jax.shard_map(
        local_fn,
        mesh=mesh,
        in_specs=(psi_spec, P("left", None, None), P("right", None, None), P()),
        out_specs=(P(), P(), psi_spec),
        check_vma=False,
    )
    return lanczos_run
```

profile of v0, /device:TPU:0, one launch (start us, length us, event | category | flops | bytes accessed | tf_op | source)
XLA Modules:
  0.0 5283.1 jit_solution(2549604663060631745)
XLA Ops:
  32.9 25.3 psum.112
  91.9 352.1 %all-to-all-done = f32[512,3,2048]{0,1,2:T(4,128)} async-done(((f32[512,3,2048]{0,1,2:T(4,128)}), f32[512,3,2048]{0,1,2:T(4,128)}, u32[]{:S(2)}, u32[]{:S(2)}) %all-to-all-start) | async-done | bytes 12582944 | tf_op jit(solution)/shard_map/all_to_all | solution.py:28
  471.3 175.8 %fusion.50 = f32[3,512,2,2,1024,1,1]{1,4,0,3,2,6,5:T(8,128)} fusion(f32[2048,3,512,1,1]{2,0,1,4,3:T(8,128)} %bitcast.303, f32[2048,2,2,1024]{0,3,2,1:T(8,128)} %all-gather.6.cloned.1.call-done), kind=kOutput, calls=%fused_computation.40 | convolution fusion | flops 154618822656 | bytes 71303168 | tf_op jit(solution)/shard_map/alc,asub->lcsub/dot_general | solution.py:32
  647.0 97.1 %fusion.35 = f32[3,2,2,512,1024]{3,0,2,1,4:T(4,128)} fusion(f32[3,512,2,2,1024,1,1]{1,4,0,3,2,6,5:T(8,128)} %fusion.50, f32[3,3,2,2,2,2]{0,1,3,2,5,4:T(4,128)S(1)} %copy.40), kind=kOutput, calls=%fused_computation.35 | convolution fusion | flops 905969664 | bytes 50332224 | tf_op jit(solution)/shard_map/lrsutv,lcsub->rtvcb/dot_general | solution.py:33
  744.1 204.5 %fusion.90 = f32[2,2,512,2048]{2,3,1,0:T(8,128)} fusion(f32[1024,3,2048]{2,0,1:T(8,128)} %param.6, f32[3,2,2,512,1024]{3,0,2,1,4:T(4,128)} %fusion.35), kind=kOutput, calls=%fused_computation.117 | convolution fusion | flops 154618822656 | bytes 67108864 | tf_op jit(solution)/shard_map/rtvcb,bre->tvce/dot_general | solution.py:34
  948.7 186.4 %reduce-scatter.6.cloned.1.call-done = f32[2,2,512,1024]{2,3,1,0:T(8,128)} async-done(((f32[2,2,512,2048]{2,3,1,0:T(8,128)}), f32[2,2,512,1024]{2,3,1,0:T(8,128)}) %reduce-scatter.6.cloned.1.call-update) | async-done | bytes 8388624 | tf_op jit(solution)/shard_map/reduce_scatter | solution.py:35
  1143.7 22.4 psum.113
  1174.3 24.4 psum.114
  1207.6 23.4 psum.115
  1242.6 201.5 %all-gather.8.cloned.1.call-done = f32[2048,2,2,1024]{0,3,2,1:T(8,128)} async-done(((f32[512,2,2,1024]{0,3,2,1:T(8,128)}), f32[2048,2,2,1024]{0,3,2,1:T(8,128)}) %all-gather.8.cloned.1.call-update) | async-done | bytes 33554448 | tf_op jit(solution)/shard_map/all_gather | solution.py:31
  1444.1 176.1 %fusion.53 = f32[3,512,2,2,1024,1,1]{1,4,0,3,2,6,5:T(8,128)} fusion(f32[2048,3,512,1,1]{2,0,1,4,3:T(8,128)} %bitcast.304, f32[2048,2,2,1024]{0,3,2,1:T(8,128)} %all-gather.8.cloned.1.call-done), kind=kOutput, calls=%fused_computation.41 | convolution fusion | flops 154618822656 | bytes 71303168 | tf_op jit(solution)/shard_map/alc,asub->lcsub/dot_general | solution.py:32
  1620.2 96.9 %fusion.38 = f32[3,2,2,512,1024]{3,0,2,1,4:T(4,128)} fusion(f32[3,512,2,2,1024,1,1]{1,4,0,3,2,6,5:T(8,128)} %fusion.53, f32[3,3,2,2,2,2]{0,1,3,2,5,4:T(4,128)S(1)} %copy.40), kind=kOutput, calls=%fused_computation.36 | convolution fusion | flops 905969664 | bytes 50332224 | tf_op jit(solution)/shard_map/lrsutv,lcsub->rtvcb/dot_general | solution.py:33
  1717.1 204.8 %fusion.95 = f32[2,2,512,2048]{2,3,1,0:T(8,128)} fusion(f32[1024,3,2048]{2,0,1:T(8,128)} %param.6, f32[3,2,2,512,1024]{3,0,2,1,4:T(4,128)} %fusion.38), kind=kOutput, calls=%fused_computation.118 | convolution fusion | flops 154618822656 | bytes 67108864 | tf_op jit(solution)/shard_map/rtvcb,bre->tvce/dot_general | solution.py:34
  1922.0 186.4 %reduce-scatter.8.cloned.1.call-done = f32[2,2,512,1024]{2,3,1,0:T(8,128)} async-done(((f32[2,2,512,2048]{2,3,1,0:T(8,128)}), f32[2,2,512,1024]{2,3,1,0:T(8,128)}) %reduce-scatter.8.cloned.1.call-update) | async-done | bytes 8388624 | tf_op jit(solution)/shard_map/reduce_scatter | solution.py:35
  2120.1 22.2 psum.116
  2156.0 23.9 psum.117
  2197.1 23.2 psum.118
  2228.7 201.4 %all-gather.10.cloned.1.call-done = f32[2048,2,2,1024]{0,3,2,1:T(8,128)} async-done(((f32[512,2,2,1024]{0,3,2,1:T(8,128)}), f32[2048,2,2,1024]{0,3,2,1:T(8,128)}) %all-gather.10.cloned.1.call-update) | async-done | bytes 33554448 | tf_op jit(solution)/shard_map/all_gather | solution.py:31
  2430.1 175.9 %fusion.56 = f32[3,512,2,2,1024,1,1]{1,4,0,3,2,6,5:T(8,128)} fusion(f32[2048,3,512,1,1]{2,0,1,4,3:T(8,128)} %bitcast.305, f32[2048,2,2,1024]{0,3,2,1:T(8,128)} %all-gather.10.cloned.1.call-done), kind=kOutput, calls=%fused_computation.42 | convolution fusion | flops 154618822656 | bytes 71303168 | tf_op jit(solution)/shard_map/alc,asub->lcsub/dot_general | solution.py:32
  2606.0 96.9 %fusion.41 = f32[3,2,2,512,1024]{3,0,2,1,4:T(4,128)} fusion(f32[3,512,2,2,1024,1,1]{1,4,0,3,2,6,5:T(8,128)} %fusion.56, f32[3,3,2,2,2,2]{0,1,3,2,5,4:T(4,128)S(1)} %copy.40), kind=kOutput, calls=%fused_computation.37 | convolution fusion | flops 905969664 | bytes 50332224 | tf_op jit(solution)/shard_map/lrsutv,lcsub->rtvcb/dot_general | solution.py:33
  2702.9 204.8 %fusion.100 = f32[2,2,512,2048]{2,3,1,0:T(8,128)} fusion(f32[1024,3,2048]{2,0,1:T(8,128)} %param.6, f32[3,2,2,512,1024]{3,0,2,1,4:T(4,128)} %fusion.41), kind=kOutput, calls=%fused_computation.119 | convolution fusion | flops 154618822656 | bytes 67108864 | tf_op jit(solution)/shard_map/rtvcb,bre->tvce/dot_general | solution.py:34
  2907.7 186.4 %reduce-scatter.10.cloned.1.call-done = f32[2,2,512,1024]{2,3,1,0:T(8,128)} async-done(((f32[2,2,512,2048]{2,3,1,0:T(8,128)}), f32[2,2,512,1024]{2,3,1,0:T(8,128)}) %reduce-scatter.10.cloned.1.call-update) | async-done | bytes 8388624 | tf_op jit(solution)/shard_map/reduce_scatter | solution.py:35
  3109.6 22.2 psum.119
  3132.4 18.7 multiply_reduce_fusion.14
  3153.0 23.9 psum.120
  3177.6 18.7 multiply_reduce_fusion.11
  3196.3 23.2 psum.121
  3227.9 201.4 %all-gather.12.cloned.1.call-done = f32[2048,2,2,1024]{0,3,2,1:T(8,128)} async-done(((f32[512,2,2,1024]{0,3,2,1:T(8,128)}), f32[2048,2,2,1024]{0,3,2,1:T(8,128)}) %all-gather.12.cloned.1.call-update) | async-done | bytes 33554448 | tf_op jit(solution)/shard_map/all_gather | solution.py:31
  3429.3 176.0 %fusion.59 = f32[3,512,2,2,1024,1,1]{1,4,0,3,2,6,5:T(8,128)} fusion(f32[2048,3,512,1,1]{2,0,1,4,3:T(8,128)} %bitcast.306, f32[2048,2,2,1024]{0,3,2,1:T(8,128)} %all-gather.12.cloned.1.call-done), kind=kOutput, calls=%fused_computation.43 | convolution fusion | flops 154618822656 | bytes 71303168 | tf_op jit(solution)/shard_map/alc,asub->lcsub/dot_general | solution.py:32
  3605.2 97.1 %fusion.44 = f32[3,2,2,512,1024]{3,0,2,1,4:T(4,128)} fusion(f32[3,512,2,2,1024,1,1]{1,4,0,3,2,6,5:T(8,128)} %fusion.59, f32[3,3,2,2,2,2]{0,1,3,2,5,4:T(4,128)S(1)} %copy.40), kind=kOutput, calls=%fused_computation.38 | convolution fusion | flops 905969664 | bytes 50332224 | tf_op jit(solution)/shard_map/lrsutv,lcsub->rtvcb/dot_general | solution.py:33
  3702.3 204.5 %fusion.105 = f32[2,2,512,2048]{2,3,1,0:T(8,128)} fusion(f32[1024,3,2048]{2,0,1:T(8,128)} %param.6, f32[3,2,2,512,1024]{3,0,2,1,4:T(4,128)} %fusion.44), kind=kOutput, calls=%fused_computation.120 | convolution fusion | flops 154618822656 | bytes 67108864 | tf_op jit(solution)/shard_map/rtvcb,bre->tvce/dot_general | solution.py:34
  3906.9 186.4 %reduce-scatter.12.cloned.1.call-done = f32[2,2,512,1024]{2,3,1,0:T(8,128)} async-done(((f32[2,2,512,2048]{2,3,1,0:T(8,128)}), f32[2,2,512,1024]{2,3,1,0:T(8,128)}) %reduce-scatter.12.cloned.1.call-update) | async-done | bytes 8388624 | tf_op jit(solution)/shard_map/reduce_scatter | solution.py:35
  4112.4 22.2 psum.122
  4135.2 21.8 multiply_reduce_fusion.10
  4159.6 23.9 psum.123
  4184.1 22.2 multiply_reduce_fusion.6
  4206.3 23.2 psum.124
  4237.9 201.4 %all-gather.14.cloned.1.call-done = f32[2048,2,2,1024]{0,3,2,1:T(8,128)} async-done(((f32[512,2,2,1024]{0,3,2,1:T(8,128)}), f32[2048,2,2,1024]{0,3,2,1:T(8,128)}) %all-gather.14.cloned.1.call-update) | async-done | bytes 33554448 | tf_op jit(solution)/shard_map/all_gather | solution.py:31
  4439.3 176.1 %fusion.62 = f32[3,512,2,2,1024,1,1]{1,4,0,3,2,6,5:T(8,128)} fusion(f32[2048,3,512,1,1]{2,0,1,4,3:T(8,128)} %bitcast.307, f32[2048,2,2,1024]{0,3,2,1:T(8,128)} %all-gather.14.cloned.1.call-done), kind=kOutput, calls=%fused_computation.44 | convolution fusion | flops 154618822656 | bytes 71303168 | tf_op jit(solution)/shard_map/alc,asub->lcsub/dot_general | solution.py:32
  4615.4 96.9 %fusion.47 = f32[3,2,2,512,1024]{3,0,2,1,4:T(4,128)} fusion(f32[3,512,2,2,1024,1,1]{1,4,0,3,2,6,5:T(8,128)} %fusion.62, f32[3,3,2,2,2,2]{0,1,3,2,5,4:T(4,128)S(1)} %copy.40), kind=kOutput, calls=%fused_computation.39 | convolution fusion | flops 905969664 | bytes 50332224 | tf_op jit(solution)/shard_map/lrsutv,lcsub->rtvcb/dot_general | solution.py:33
  4712.3 204.6 %fusion.110 = f32[2,2,512,2048]{2,3,1,0:T(8,128)} fusion(f32[1024,3,2048]{2,0,1:T(8,128)} %param.6, f32[3,2,2,512,1024]{3,0,2,1,4:T(4,128)} %fusion.47), kind=kOutput, calls=%fused_computation.121 | convolution fusion | flops 154618822656 | bytes 67108864 | tf_op jit(solution)/shard_map/rtvcb,bre->tvce/dot_general | solution.py:34
  4917.0 186.5 %reduce-scatter.14.cloned.1.call-done = f32[2,2,512,1024]{2,3,1,0:T(8,128)} async-done(((f32[2,2,512,2048]{2,3,1,0:T(8,128)}), f32[2,2,512,1024]{2,3,1,0:T(8,128)}) %reduce-scatter.14.cloned.1.call-update) | async-done | bytes 8388624 | tf_op jit(solution)/shard_map/reduce_scatter | solution.py:35
  5103.4 18.5 fusion.69
  5125.1 22.2 psum.125
  5148.0 25.2 multiply_reduce_fusion.1
  5180.2 23.9 psum.126
  5204.8 25.1 multiply_reduce_fusion
  5229.9 23.2 psum.127
  (63 shorter events, 263.3 us)
Async XLA Ops:
  7.2 464.1 %all-gather.6.cloned.1.call-start = ((), (), s32[]{:S(2)}) async-start(), calls=%async_computation.6 | async-start | bytes 41943040 | tf_op jit(solution)/shard_map/all_gather | solution.py:31
  84.5 7.3 copy-start
  84.5 359.5 %all-to-all-start = ((f32[512,3,2048]{0,1,2:T(4,128)}), f32[512,3,2048]{0,1,2:T(4,128)}, u32[]{:S(2)}, u32[]{:S(2)}) async-start(f32[512,3,2048]{0,1,2:T(4,128)} %copy.36), calls=%async_computation | async-start | bytes 33554432 | tf_op jit(solution)/shard_map/all_to_all | solution.py:28
  91.7 1043.5 %reduce-scatter.6.cloned.1.call-start = ((), (), s32[]{:S(2)}) async-start(), calls=%async_computation.7 | async-start | bytes 25165824 | tf_op jit(solution)/shard_map/reduce_scatter | solution.py:35
  948.7 495.4 %all-gather.8.cloned.1.call-start = ((), (), s32[]{:S(2)}) async-start(), calls=%async_computation.8 | async-start | bytes 41943040 | tf_op jit(solution)/shard_map/all_gather | solution.py:31
  1242.5 865.8 %reduce-scatter.8.cloned.1.call-start = ((), (), s32[]{:S(2)}) async-start(), calls=%async_computation.9 | async-start | bytes 25165824 | tf_op jit(solution)/shard_map/reduce_scatter | solution.py:35
  1921.9 508.2 %all-gather.10.cloned.1.call-start = ((), (), s32[]{:S(2)}) async-start(), calls=%async_computation.10 | async-start | bytes 41943040 | tf_op jit(solution)/shard_map/all_gather | solution.py:31
  2228.6 865.5 %reduce-scatter.10.cloned.1.call-start = ((), (), s32[]{:S(2)}) async-start(), calls=%async_computation.11 | async-start | bytes 25165824 | tf_op jit(solution)/shard_map/reduce_scatter | solution.py:35
  2907.7 521.6 %all-gather.12.cloned.1.call-start = ((), (), s32[]{:S(2)}) async-start(), calls=%async_computation.12 | async-start | bytes 41943040 | tf_op jit(solution)/shard_map/all_gather | solution.py:31
  3227.8 865.5 %reduce-scatter.12.cloned.1.call-start = ((), (), s32[]{:S(2)}) async-start(), calls=%async_computation.13 | async-start | bytes 25165824 | tf_op jit(solution)/shard_map/reduce_scatter | solution.py:35
  3906.9 532.4 %all-gather.14.cloned.1.call-start = ((), (), s32[]{:S(2)}) async-start(), calls=%async_computation.14 | async-start | bytes 41943040 | tf_op jit(solution)/shard_map/all_gather | solution.py:31
  4237.8 865.6 %reduce-scatter.14.cloned.1.call-start = ((), (), s32[]{:S(2)}) async-start(), calls=%async_computation.15 | async-start | bytes 25165824 | tf_op jit(solution)/shard_map/reduce_scatter | solution.py:35
Sparse Core Ops, SparseCore 0:
  66.7 370.2 all-gather.5
  948.8 186.2 reduce-scatter.5
  1242.7 201.3 all-gather.7
  1922.0 186.2 reduce-scatter.7
  2228.7 201.2 all-gather.9
  2907.8 186.2 reduce-scatter.9
  3228.0 201.2 all-gather.11
  3907.0 186.3 reduce-scatter.11
  4238.0 201.2 all-gather.13
  4917.1 186.3 reduce-scatter.13
where the time goes:
time: 5290 us; the launch traced here: 5280 us
  matrix products  2390 us (45%)
  waiting for transfers between devices  2090 us (40%)
  blocking collectives  373 us (7%)
  other arithmetic  318 us (6%)
  local copies, waits for them, and re-layouts  87.8 us (2%)
    dot_general x5, matrix products, apply_ham(): jnp.einsum('rtvcb,bre->tvce', stage_two, env_right, precision=PREC_MODE,...  1020 us
    reduce_scatter x5, waiting for transfers between devices, apply_ham(): lax.psum_scatter(part_out, 'right', scatter_dimension=3, tiled=True)  932 us
    dot_general x5, matrix products, apply_ham(): jnp.einsum('alc,asub->lcsub', left_full, vec_full, precision=PREC_MODE, p...  880 us
    all_gather x5, waiting for transfers between devices, apply_ham(): vec_full = lax.all_gather(in_vec, 'left', axis=0, tiled=True)  806 us
    dot_general x5, matrix products, apply_ham(): jnp.einsum('lrsutv,lcsub->rtvcb', mpo_pair, stage_one, precision=PREC_MOD...  485 us
    all_to_all x1, waiting for transfers between devices, local_fn(): left_full = lax.all_to_all(env_left, 'left', 2, 0, tiled=True)  352 us
    psum x10, blocking collectives, global_dots(): return lax.psum(local_dots, BOTH_AXES)  231 us
    reduce_sum x10, other arithmetic, global_dots(): jnp.sum(basis_vec * residual)  153 us
  transfers between devices with their start and end apart: 11, of which 10 were waited for; matrix products, arithmetic and copies ran while one was open for 1% of the time, Pallas kernels for 0%

commit v1 on v0

v1 whole, which is shorter than its diff:
```python
import functools
import math
import jax
import jax.numpy as jnp
from jax import lax
from jax.experimental import pallas as pl
from jax.experimental.pallas import tpu as pltpu
from jax.sharding import PartitionSpec as P

KRYLOV_STEPS = 5
LANES = 128
PHYS = 4
BONDS = 3
AHEAD = 2
VMEM_BYTES = 66 * 1000 * 1000
F32 = jnp.float32
BF16 = jnp.bfloat16
ANY = pl.BlockSpec(memory_space=pltpu.HBM)
IN_VMEM = pl.BlockSpec(memory_space=pltpu.VMEM)
IN_SMEM = pl.BlockSpec(memory_space=pltpu.SMEM)
MESH = pl.DeviceIdType.MESH


def split3(x):
    hi = x.astype(BF16)
    rest = x - hi.astype(F32)
    mid = rest.astype(BF16)
    return hi, mid, (rest - mid.astype(F32)).astype(BF16)


def dot6(lhs, rhs):
    def one(p, q):
        return jnp.dot(lhs(p), rhs(q), preferred_element_type=F32)

    return one(2, 0) + one(0, 2) + one(1, 1) + one(1, 0) + one(0, 1) + one(0, 0)


def barrier(peers):
    sem = pltpu.get_barrier_semaphore()
    for peer in peers:
        pl.semaphore_signal(sem, inc=1, device_id=peer, device_id_type=MESH)
    pl.semaphore_wait(sem, len(peers))


def params(collective_id=None):
    return pltpu.CompilerParams(
        collective_id=collective_id,
        has_side_effects=collective_id is not None,
        vmem_limit_bytes=VMEM_BYTES,
    )


def split_matrix(x):
    rows, cols = x.shape
    block = 128

    def body(x_ref, o_ref):
        for p, part in enumerate(split3(x_ref[...])):
            o_ref[p] = part

    return pl.pallas_call(
        body,
        grid=(rows // block,),
        out_shape=jax.ShapeDtypeStruct((3, rows, cols), BF16),
        in_specs=[pl.BlockSpec((block, cols), lambda i: (i, 0))],
        out_specs=pl.BlockSpec((3, block, cols), lambda i: (0, i, 0)),
        compiler_params=params(),
    )(x)


def first_body(
    u, inv, w, ls, t2o, vo, pb, xb, fb,
    lv, vfl, vfr, vsl, vsr, t1, t2b,
    ps, pr, xs, xr, fs, fr, lsem, lload, rload, vsem, tsem,
):
    n_chunks, na, cols = u.shape
    half = 2 * na
    left = lax.axis_index("left")
    x, core = left // 2, left % 2
    partner = {"left": 2 * x + 1 - core}
    across = {"left": 2 * (1 - x) + core}
    mine = pl.ds(pl.multiple_of(core * na, na), na)
    other = pl.ds(pl.multiple_of((1 - core) * na, na), na)
    near = pl.ds(pl.multiple_of(x * half, half), half)
    far = pl.ds(pl.multiple_of((1 - x) * half, half), half)

    def to_partner(k):
        return pltpu.make_async_remote_copy(u.at[k], pb.at[k], ps.at[k], pr.at[k], device_id=partner, device_id_type=MESH)

    def to_across(k):
        return pltpu.make_async_remote_copy(u.at[k], xb.at[k], xs.at[k], xr.at[k], device_id=across, device_id_type=MESH)

    def forward(k):
        return pltpu.make_async_remote_copy(xb.at[k], fb.at[k], fs.at[k], fr.at[k], device_id=partner, device_id_type=MESH)

    def load_l(p):
        return pltpu.make_async_copy(ls.at[p], lv.at[p], lsem.at[p])

    def load_mine(k):
        return pltpu.make_async_copy(u.at[k], vfl.at[k % 2, mine], lload.at[k % 2, 0])

    def load_partner(k):
        return pltpu.make_async_copy(pb.at[k], vfl.at[k % 2, other], lload.at[k % 2, 1])

    def load_across(k):
        return pltpu.make_async_copy(xb.at[k], vfr.at[mine], rload.at[0])

    def load_forward(k):
        return pltpu.make_async_copy(fb.at[k], vfr.at[other], rload.at[1])

    def store_v(k):
        return pltpu.make_async_copy(vfl.at[k % 2, mine], vo.at[k], vsem.at[k % 2])

    def store_t2(k):
        return pltpu.make_async_copy(t2b.at[k % 2], t2o.at[k], tsem.at[k % 2])

    barrier([partner, across])
    for k in range(n_chunks):
        to_across(k).start()
    for k in range(n_chunks):
        to_partner(k).start()
    load_mine(0).start()
    for p in range(3):
        load_l(p).start()
    to_partner(0).wait_recv()
    load_partner(0).start()
    scale = inv[0:1, 0:1]

    def split_half(src, dst, keep):
        block = 32

        @pl.loop(0, half // block)
        def _(i):
            rows = pl.ds(pl.multiple_of(i * block, block), block)
            v = src[rows, :] * scale
            if keep:
                src[rows, :] = v
            for p, part in enumerate(split3(v)):
                dst[p, rows, :] = part

    @pl.loop(0, n_chunks + AHEAD)
    def _(k):
        back = k - AHEAD

        @pl.when(back >= 0)
        def _():
            to_across(back).wait_recv()
            forward(back).start()
            load_across(back).start()

        @pl.when(k < n_chunks)
        def _():
            load_mine(k).wait()
            load_partner(k).wait()

            @pl.when(k + 1 < n_chunks)
            def _():
                @pl.when(k >= 1)
                def _():
                    store_v(k - 1).wait()

                load_mine(k + 1).start()
                to_partner(k + 1).wait_recv()
                load_partner(k + 1).start()

            split_half(vfl.at[k % 2], vsl, True)
            store_v(k).start()

            @pl.when(k == 0)
            def _():
                for p in range(3):
                    load_l(p).wait()

            @pl.loop(0, BONDS)
            def _(i):
                rows = pl.ds(pl.multiple_of(i * na, na), na)
                t1[k % (AHEAD + 1), rows, :] = dot6(lambda p: lv[p, rows, near], lambda q: vsl[q])

        @pl.when(back >= 0)
        def _():
            forward(back).wait_recv()
            load_forward(back).start()
            load_across(back).wait()
            load_forward(back).wait()
            split_half(vfr, vsr, False)
            slot = back % (AHEAD + 1)

            @pl.loop(0, BONDS)
            def _(i):
                rows = pl.ds(pl.multiple_of(i * na, na), na)
                t1[slot, rows, :] = t1[slot, rows, :] + dot6(lambda p: lv[p, rows, far], lambda q: vsr[q])

            @pl.when(back >= 2)
            def _():
                store_t2(back - 2).wait()

            block = 32

            @pl.loop(0, na // block)
            def _(i):
                base = pl.multiple_of(i * block, block)
                for r in range(BONDS):
                    for t in range(PHYS):
                        acc = None
                        for l in range(BONDS):
                            for s in range(PHYS):
                                term = w[((l * BONDS + r) * PHYS + s) * PHYS + t] * t1[slot, pl.ds(l * na + base, block), s * LANES : (s + 1) * LANES]
                                acc = term if acc is None else acc + term
                        for p, part in enumerate(split3(acc)):
                            t2b[back % 2, p, pl.ds(t * na + base, block), r * LANES : (r + 1) * LANES] = part

            store_t2(back).start()

    for k in range(max(n_chunks - 2, 0), n_chunks):
        store_v(k).wait()
        store_t2(k).wait()
    for k in range(n_chunks):
        to_across(k).wait_send()
        to_partner(k).wait_send()
        forward(k).wait_send()


def first(u, inv, w, ls, collective_id):
    n_chunks, na, cols = u.shape
    half = 2 * na
    vec = jax.ShapeDtypeStruct(u.shape, F32)
    dma = pltpu.SemaphoreType.DMA
    out = pl.pallas_call(
        first_body,
        out_shape=[jax.ShapeDtypeStruct((n_chunks, 3, PHYS * na, BONDS * LANES), BF16), vec, vec, vec, vec],
        in_specs=[ANY, IN_VMEM, IN_SMEM, ANY],
        out_specs=[ANY] * 5,
        scratch_shapes=[
            pltpu.VMEM(ls.shape, BF16),
            pltpu.VMEM((2, half, cols), F32),
            pltpu.VMEM((half, cols), F32),
            pltpu.VMEM((3, half, cols), BF16),
            pltpu.VMEM((3, half, cols), BF16),
            pltpu.VMEM((AHEAD + 1, BONDS * na, cols), F32),
            pltpu.VMEM((2, 3, PHYS * na, BONDS * LANES), BF16),
            *[dma((n_chunks,))] * 6,
            dma((3,)),
            dma((2, 2)),
            dma((2,)),
            dma((2,)),
            dma((2,)),
        ],
        compiler_params=params(collective_id),
        name="gather_first",
    )(u, inv, w, ls)
    return out[0], out[1]


def second_body(
    t2, rs, uo, sendb, recvb,
    rv, tv, ob, rb,
    ss, sr, rsem, tsem, stage, rload, osem,
):
    n_chunks, _, rows_all, k_chunk = t2.shape
    na = rows_all // PHYS
    _, k_all, wide = rv.shape[1:]
    mt = tv.shape[2]
    n_m = rows_all // mt
    per_t = na // mt
    n_n = rv.shape[0] // 2
    tiles = n_m * n_n
    per_chunk = wide // LANES
    right = lax.axis_index("right")
    peer = {"right": 1 - right}

    def load_r(h, n):
        owner = right if h else 1 - right
        col = pl.multiple_of((owner * n_n + n) * wide, wide)
        return pltpu.make_async_copy(rs.at[:, :, pl.ds(col, wide)], rv.at[h * n_n + n], rsem.at[h * n_n + n])

    def load_t(g):
        m, slot = g % n_m, g % 2
        rows = pl.ds(pl.multiple_of(m * mt, mt), mt)
        return [
            pltpu.make_async_copy(t2.at[c, :, rows], tv.at[slot, :, :, c * k_chunk : (c + 1) * k_chunk], tsem.at[slot, c])
            for c in range(n_chunks)
        ]

    def put(q):
        return pltpu.make_async_copy(ob.at[q % 3], sendb.at[q], stage.at[q % 3])

    def send(q):
        return pltpu.make_async_remote_copy(sendb.at[q], recvb.at[q], ss.at[q], sr.at[q], device_id=peer, device_id_type=MESH)

    def fetch(q):
        return pltpu.make_async_copy(recvb.at[q], rb.at[q % 2], rload.at[q % 2])

    def emit(q):
        m, n = q // n_n, q % n_n
        t, part = m // per_t, m % per_t
        rows = pl.ds(pl.multiple_of(part * mt, mt), mt)
        lanes = pl.ds(pl.multiple_of(t * LANES, LANES), LANES)
        return [
            pltpu.make_async_copy(
                ob.at[q % 3, :, c * LANES : (c + 1) * LANES],
                uo.at[n * per_chunk + c, rows, lanes],
                osem.at[q % 3, c],
            )
            for c in range(per_chunk)
        ]

    for copy in load_t(0):
        copy.start()
    for n in range(n_n):
        load_r(0, n).start()
    for n in range(n_n):
        load_r(1, n).start()
    barrier([peer])

    def tile(h, q, slot3):
        g = h * n_m + q // n_n

        @pl.when(q % n_n == 0)
        def _():
            for copy in load_t(g):
                copy.wait()

            @pl.when(g + 1 < 2 * n_m)
            def _():
                for copy in load_t(g + 1):
                    copy.start()

        for n in range(n_n):

            @pl.when(q == n)
            def _():
                load_r(h, n).wait()

        ob[slot3] = dot6(lambda p: tv[g % 2, p], lambda p: rv[h * n_n + q % n_n, p])

    @pl.loop(0, tiles)
    def _(q):
        @pl.when(q >= 1)
        def _():
            put(q - 1).wait()
            send(q - 1).start()

        tile(0, q, q % 3)
        put(q).start()

        @pl.when(q == 0)
        def _():
            pass

    put(tiles - 1).wait()
    send(tiles - 1).start()

    def finish(q):
        fetch(q).wait()
        ob[q % 3] = ob[q % 3] + rb[q % 2]
        for copy in emit(q):
            copy.start()

    @pl.loop(0, tiles)
    def _(q):
        @pl.when(q >= 1)
        def _():
            send(q - 1).wait_recv()
            fetch(q - 1).start()

        @pl.when(q >= 3)
        def _():
            for copy in emit(q - 3):
                copy.wait()

        tile(1, q, q % 3)

        @pl.when(q >= 1)
        def _():
            finish(q - 1)

    send(tiles - 1).wait_recv()
    fetch(tiles - 1).start()
    finish(tiles - 1)
    for q in range(max(tiles - 3, 0), tiles):
        for copy in emit(q):
            copy.wait()
    for q in range(tiles):
        send(q).wait_send()


def second(t2, rs, n_chunks, na, collective_id):
    _, k_all, nb = rs.shape
    wide = min(512, nb // 2)
    n_n = nb // 2 // wide
    mt = min(256, na)
    tiles = PHYS * na // mt * n_n
    per_chunk = wide // LANES
    dma = pltpu.SemaphoreType.DMA
    block = jax.ShapeDtypeStruct((tiles, mt, wide), F32)
    out = pl.pallas_call(
        second_body,
        out_shape=[jax.ShapeDtypeStruct((n_chunks, na, PHYS * LANES), F32), block, block],
        in_specs=[ANY, ANY],
        out_specs=[ANY] * 3,
        scratch_shapes=[
            pltpu.VMEM((2 * n_n, 3, k_all, wide), BF16),
            pltpu.VMEM((2, 3, mt, k_all), BF16),
            pltpu.VMEM((3, mt, wide), F32),
            pltpu.VMEM((2, mt, wide), F32),
            dma((tiles,)),
            dma((tiles,)),
            dma((2 * n_n,)),
            dma((2, n_chunks)),
            dma((3,)),
            dma((2,)),
            dma((3, per_chunk)),
        ],
        compiler_params=params(collective_id),
        name="second_scatter",
    )(t2, rs)
    return out[0]


def third_body(n_basis, n_right, n_left, *refs):
    u, *refs = refs
    vs, refs = refs[:n_basis], refs[n_basis:]
    if n_basis:
        uo, inv, alpha, beta, *refs = refs
    else:
        inv, *refs = refs
    ub, refs = refs[0], refs[1:]
    vb, refs = refs[:n_basis], refs[n_basis:]
    sbuf, rbuf, ssem, rsem, load, osem = refs
    n_chunks, na, cols = u.shape
    n_dev = n_right * n_left
    me = lax.axis_index("right") * n_left + lax.axis_index("left")
    block = 32

    def place(d):
        return {"right": d // n_left, "left": d % n_left}

    def loads(c):
        return [pltpu.make_async_copy(u.at[c], ub.at[c], load.at[0, c])] + [
            pltpu.make_async_copy(v.at[c], b.at[c], load.at[i + 1, c]) for i, (v, b) in enumerate(zip(vs, vb))
        ]

    for c in range(n_chunks):
        for copy in loads(c):
            copy.start()
    peers = [(me + k) % n_dev for k in range(1, n_dev)]
    barrier([place(d) for d in peers])

    def fold(x):
        return jnp.sum(x.reshape(block // 8, 8, cols), axis=0)

    def everywhere(step, sums):
        rows = [jnp.sum(jnp.sum(s.reshape(8, cols // LANES, LANES), axis=1), axis=0, keepdims=True) for s in sums]
        sbuf[step] = jnp.concatenate(rows + [jnp.zeros((8 - len(rows), LANES), F32)], axis=0)
        rbuf[step, me] = sbuf[step]

        def copy(k, to):
            return pltpu.make_async_remote_copy(
                sbuf.at[step], rbuf.at[step, to], ssem.at[step, k], rsem.at[step, to],
                device_id=place(peers[k]), device_id_type=MESH,
            )

        for k in range(n_dev - 1):
            copy(k, me).start()
        for k in range(n_dev - 1):
            copy(k, peers[k]).wait_recv()
        for k in range(n_dev - 1):
            copy(k, me).wait_send()
        total = rbuf[step, 0]
        for d in range(1, n_dev):
            total = total + rbuf[step, d]
        return [jnp.sum(total[i : i + 1, :]) for i in range(len(rows))]

    zero = jnp.zeros((8, cols), F32)

    def sweep(n_sums, per_block, before=None, after=None):
        @functools.partial(lax.fori_loop, 0, n_chunks, init_val=(zero,) * n_sums)
        def sums(c, carry):
            if before is not None:
                before(c)

            def inner(i, carry):
                rows = pl.ds(pl.multiple_of(i * block, block), block)
                return tuple(a + b for a, b in zip(carry, per_block(c, rows)))

            carry = lax.fori_loop(0, na // block, inner, carry)
            if after is not None:
                after(c)
            return carry

        return sums

    def arrive(c):
        for copy in loads(c):
            copy.wait()

    if not n_basis:
        def square(c, rows):
            x = ub[c, rows, :]
            return (fold(x * x),)

        (total,) = everywhere(0, sweep(1, square, before=arrive))
        inv[...] = 1.0 / jnp.sqrt(jnp.full((8, LANES), total, F32))
        return

    def overlaps(c, rows):
        x = ub[c, rows, :]
        return tuple(fold(b[c, rows, :] * x) for b in vb)

    once = everywhere(0, sweep(n_basis, overlaps, before=arrive))
    alpha[...] = jnp.full((8, LANES), once[-1], F32)

    def project(c, rows, coeffs):
        x = ub[c, rows, :]
        basis = [b[c, rows, :] for b in vb]
        for coeff, v in zip(coeffs, basis):
            x = x - coeff * v
        ub[c, rows, :] = x
        return x, basis

    def project_once(c, rows):
        x, basis = project(c, rows, once)
        return tuple(fold(v * x) for v in basis)

    twice = everywhere(1, sweep(n_basis, project_once))

    def project_twice(c, rows):
        x, _ = project(c, rows, twice)
        return (fold(x * x),)

    def store(c):
        return pltpu.make_async_copy(ub.at[c], uo.at[c], osem.at[c])

    (total,) = everywhere(2, sweep(1, project_twice, after=lambda c: store(c).start()))
    norm = jnp.sqrt(jnp.full((8, LANES), total, F32))
    beta[...] = norm
    inv[...] = 1.0 / norm
    for c in range(n_chunks):
        store(c).wait()


def third(u, basis, mesh, collective_id):
    n_chunks = u.shape[0]
    n_right, n_left = mesh.shape["right"], mesh.shape["left"]
    n_dev = n_right * n_left
    small = jax.ShapeDtypeStruct((8, LANES), F32)
    vec = jax.ShapeDtypeStruct(u.shape, F32)
    dma = pltpu.SemaphoreType.DMA
    return pl.pallas_call(
        functools.partial(third_body, len(basis), n_right, n_left),
        out_shape=[vec, small, small, small] if basis else [small],
        in_specs=[ANY] * (1 + len(basis)),
        out_specs=[ANY, IN_VMEM, IN_VMEM, IN_VMEM] if basis else [IN_VMEM],
        scratch_shapes=[
            *[pltpu.VMEM(u.shape, F32)] * (1 + len(basis)),
            pltpu.VMEM((3, 8, LANES), F32),
            pltpu.VMEM((3, n_dev, 8, LANES), F32),
            dma((3, n_dev)),
            dma((3, n_dev)),
            dma((1 + len(basis), n_chunks)),
            dma((n_chunks,)),
        ],
        compiler_params=params(collective_id),
        name="orthogonalise",
    )(u, *basis)


def solution(mesh):
    n_devices = mesh.shape["left"] * mesh.shape["right"]
    psi_spec = P("left", None, None, "right")

    def local_fn(psi_loc, env_left, env_right, mpo_pair):
        na, nbl = psi_loc.shape[0], psi_loc.shape[3]
        n_chunks = nbl // LANES
        ls = split_matrix(jnp.transpose(env_left, (1, 0, 2)).reshape(BONDS * na, -1))
        right_rows = env_right.reshape(n_chunks, LANES, BONDS, -1).transpose(0, 2, 1, 3)
        rs = split_matrix(right_rows.reshape(BONDS * nbl, -1))
        w = mpo_pair.reshape(-1)
        u = psi_loc.reshape(na, PHYS, n_chunks, LANES).transpose(2, 0, 1, 3).reshape(n_chunks, na, PHYS * LANES)
        (inv,) = third(u, [], mesh, 0)
        basis, alpha_list, beta_list = [], [], []
        for step_idx in range(KRYLOV_STEPS):
            t2, v = first(u, inv, w, ls, 3 * step_idx + 1)
            basis.append(v)
            hv = second(t2, rs, n_chunks, na, 3 * step_idx + 2)
            u, inv, alpha, beta = third(hv, basis, mesh, 3 * step_idx + 3)
            alpha_list.append(alpha[0, 0])
            beta_list.append(beta[0, 0])
        out_scale = math.sqrt(float(psi_loc.size * n_devices))
        last = u.reshape(n_chunks, na, PHYS, LANES).transpose(1, 2, 0, 3).reshape(psi_loc.shape)
        return jnp.stack(alpha_list), jnp.stack(beta_list), last * inv[0, 0] * out_scale

    return jax.shard_map(
        local_fn,
        mesh=mesh,
        in_specs=(psi_spec, P("left", None, None), P("right", None, None), P()),
        out_specs=(P(), P(), psi_spec),
        check_vma=False,
    )
```

time: 5290 us -> 2540 us (0.48)
  Pallas kernels: 0 us -> 2420 us
  matrix products: 2390 us -> 0 us
  waiting for transfers between devices: 2090 us -> 0 us
  blocking collectives: 373 us -> 0 us
  other arithmetic: 318 us -> 9.22 us
    pallas_call x0 -> x18, Pallas kernels: none -> 2420 us  [the longest x5 1240 us: first(): pl.pallas_call(first_body, out_shape=[jax.ShapeDtypeStruct((n_chunks, 3,...]
    dot_general x15 -> x0, matrix products: 2390 us -> none  [the longest x5 1020 us: apply_ham(): jnp.einsum('rtvcb,bre->tvce', stage_two, env_right, precision=PREC_MODE,...]
    reduce_scatter x5 -> x0, waiting for transfers between devices: 932 us -> none  [apply_ham(): lax.psum_scatter(part_out, 'right', scatter_dimension=3, tiled=True)]
    all_gather x5 -> x0, waiting for transfers between devices: 806 us -> none  [apply_ham(): vec_full = lax.all_gather(in_vec, 'left', axis=0, tiled=True)]
    psum x16 -> x0, blocking collectives: 373 us -> none  [the longest x10 231 us: global_dots(): return lax.psum(local_dots, BOTH_AXES)]
    all_to_all x1 -> x0, waiting for transfers between devices: 352 us -> none  [local_fn(): left_full = lax.all_to_all(env_left, 'left', 2, 0, tiled=True)]
    reduce_sum x16 -> x0, other arithmetic: 257 us -> none  [the longest x10 153 us: global_dots(): jnp.sum(basis_vec * residual)]
  transfers between devices with their start and end apart: 11 -> 0, of which waited for: 10 -> 0; matrix products, arithmetic and copies ran while one was open for 1% -> 0% of each run, Pallas kernels for 0% -> 0%
where the time goes in v1:
time: 2540 us; the launch traced here: 2530 us
  Pallas kernels  2420 us (95%)
  local copies, waits for them, and re-layouts  102 us (4%)
    pallas_call x5, Pallas kernels, first(): pl.pallas_call(first_body, out_shape=[jax.ShapeDtypeStruct((n_chunks, 3,...  1240 us
    pallas_call x5, Pallas kernels, second(): pl.pallas_call(second_body, out_shape=[jax.ShapeDtypeStruct((n_chunks, na...  975 us
    pallas_call x6, Pallas kernels, third(): pl.pallas_call(functools.partial(third_body, len(basis), n_right, n_left)...  162 us

profile of v1, /device:TPU:0, one launch (start us, length us, event | category | flops | bytes accessed | tf_op | source)
XLA Modules:
  0.0 2529.4 jit_solution(17561201878199413168)
XLA Ops:
  0.6 1.0 copy.11
  1.6 0.7 reshape.36.w
  2.3 11.5 reshape.34
  13.8 8.8 copy.15
  22.5 10.3 reshape.35.refs_0_.u
  32.8 10.8 orthogonalise.6.inv
  43.6 15.0 shard_map.67.ls
  58.6 17.4 copy.12
  76.0 29.2 %shard_map.68.rs = bf16[3,3072,2048]{2,1,0:T(8,128)(2,1)} custom-call(f32[3072,2048]{1,0:T(8,128)} %bitcast.24), custom_call_target="tpu_custom_call" | custom-call | tf_op jit(solution)/shard_map/pallas_call | solution.py:61
  105.2 246.8 %gather_first.5 = (bf16[8,3,2048,384]{3,2,1,0:T(8,128)(2,1)}, f32[8,512,512]{2,1,0:T(8,128)}, f32[8,512,512]{2,1,0:T(8,128)}, f32[8,512,512]{2,1,0:T(8,128)}, f32[8,512,512]{2,1,0:T(8,128)}) custom-call(f32[8,512,512]{2,1,0:T(8,128)} %reshape.35.refs_0_.u, f32[8,128]{1,0:T(8,128)} %orthogonalise.6.inv, f32[144]{0:T(256)} %reshape.36.w, ...), custom_call_target="tpu_custom_call" | custom-call | tf_op jit(solution)/shard_map/gather_first/pallas_call | solution.py:228
  352.0 195.0 %second_scatter.5 = (f32[8,512,512]{2,1,0:T(8,128)}, f32[16,256,512]{2,1,0:T(8,128)}, f32[16,256,512]{2,1,0:T(8,128)}) custom-call(bf16[8,3,2048,384]{3,2,1,0:T(8,128)(2,1)} %get-tuple-element.38.t2, bf16[3,3072,2048]{2,1,0:T(8,128)(2,1)} %shard_map.68.rs), custom_call_target="tpu_custom_call" | custom-call | tf_op jit(solution)/shard_map/second_scatter/pallas_call | solution.py:396
  547.0 22.3 orthogonalise.7
  569.3 1.2 slice.38
  570.4 1.2 slice.33
  571.6 246.9 %gather_first.6 = (bf16[8,3,2048,384]{3,2,1,0:T(8,128)(2,1)}, f32[8,512,512]{2,1,0:T(8,128)}, f32[8,512,512]{2,1,0:T(8,128)}, f32[8,512,512]{2,1,0:T(8,128)}, f32[8,512,512]{2,1,0:T(8,128)}) custom-call(f32[8,512,512]{2,1,0:T(8,128)} %get-tuple-element.42.u, f32[8,128]{1,0:T(8,128)} %get-tuple-element.43.inv, f32[144]{0:T(256)} %reshape.36.w, ...), custom_call_target="tpu_custom_call" | custom-call | tf_op jit(solution)/shard_map/gather_first/pallas_call | solution.py:228
  818.6 194.9 %second_scatter.6 = (f32[8,512,512]{2,1,0:T(8,128)}, f32[16,256,512]{2,1,0:T(8,128)}, f32[16,256,512]{2,1,0:T(8,128)}) custom-call(bf16[8,3,2048,384]{3,2,1,0:T(8,128)(2,1)} %get-tuple-element.44.t2, bf16[3,3072,2048]{2,1,0:T(8,128)(2,1)} %shard_map.68.rs), custom_call_target="tpu_custom_call" | custom-call | tf_op jit(solution)/shard_map/second_scatter/pallas_call | solution.py:396
  1013.5 26.0 %orthogonalise.8 = (f32[8,512,512]{2,1,0:T(8,128)}, f32[8,128]{1,0:T(8,128)}, f32[8,128]{1,0:T(8,128)}, f32[8,128]{1,0:T(8,128)}) custom-call(f32[8,512,512]{2,1,0:T(8,128)} %get-tuple-element.45.refs_0_, f32[8,512,512]{2,1,0:T(8,128)} %get-tuple-element.40.refs_1_, f32[8,512,512]{2,1,0:T(8,128)} %get-tuple-element.46.refs_2_), custom_call_target="tpu_custom_call" | custom-call | tf_op jit(solution)/shard_map/orthogonalise/pallas_call | solution.py:549
  1039.5 1.2 slice.39
  1040.8 1.2 slice.34
  1041.9 247.0 %gather_first.7 = (bf16[8,3,2048,384]{3,2,1,0:T(8,128)(2,1)}, f32[8,512,512]{2,1,0:T(8,128)}, f32[8,512,512]{2,1,0:T(8,128)}, f32[8,512,512]{2,1,0:T(8,128)}, f32[8,512,512]{2,1,0:T(8,128)}) custom-call(f32[8,512,512]{2,1,0:T(8,128)} %get-tuple-element.48.u, f32[8,128]{1,0:T(8,128)} %get-tuple-element.49.inv, f32[144]{0:T(256)} %reshape.36.w, ...), custom_call_target="tpu_custom_call" | custom-call | tf_op jit(solution)/shard_map/gather_first/pallas_call | solution.py:228
  1289.0 194.9 %second_scatter.7 = (f32[8,512,512]{2,1,0:T(8,128)}, f32[16,256,512]{2,1,0:T(8,128)}, f32[16,256,512]{2,1,0:T(8,128)}) custom-call(bf16[8,3,2048,384]{3,2,1,0:T(8,128)(2,1)} %get-tuple-element.50.t2, bf16[3,3072,2048]{2,1,0:T(8,128)(2,1)} %shard_map.68.rs), custom_call_target="tpu_custom_call" | custom-call | tf_op jit(solution)/shard_map/second_scatter/pallas_call | solution.py:396
  1483.9 30.1 %orthogonalise.9 = (f32[8,512,512]{2,1,0:T(8,128)}, f32[8,128]{1,0:T(8,128)}, f32[8,128]{1,0:T(8,128)}, f32[8,128]{1,0:T(8,128)}) custom-call(f32[8,512,512]{2,1,0:T(8,128)} %get-tuple-element.51.refs_0_, f32[8,512,512]{2,1,0:T(8,128)} %get-tuple-element.40.refs_1_, f32[8,512,512]{2,1,0:T(8,128)} %get-tuple-element.46.refs_2_, ...), custom_call_target="tpu_custom_call" | custom-call | tf_op jit(solution)/shard_map/orthogonalise/pallas_call | solution.py:549
  1514.0 1.2 slice.40
  1515.2 1.3 slice.35
  1516.5 247.1 %gather_first.8 = (bf16[8,3,2048,384]{3,2,1,0:T(8,128)(2,1)}, f32[8,512,512]{2,1,0:T(8,128)}, f32[8,512,512]{2,1,0:T(8,128)}, f32[8,512,512]{2,1,0:T(8,128)}, f32[8,512,512]{2,1,0:T(8,128)}) custom-call(f32[8,512,512]{2,1,0:T(8,128)} %get-tuple-element.54.u, f32[8,128]{1,0:T(8,128)} %get-tuple-element.55.inv, f32[144]{0:T(256)} %reshape.36.w, ...), custom_call_target="tpu_custom_call" | custom-call | tf_op jit(solution)/shard_map/gather_first/pallas_call | solution.py:228
  1763.6 194.9 %second_scatter.8 = (f32[8,512,512]{2,1,0:T(8,128)}, f32[16,256,512]{2,1,0:T(8,128)}, f32[16,256,512]{2,1,0:T(8,128)}) custom-call(bf16[8,3,2048,384]{3,2,1,0:T(8,128)(2,1)} %get-tuple-element.56.t2, bf16[3,3072,2048]{2,1,0:T(8,128)(2,1)} %shard_map.68.rs), custom_call_target="tpu_custom_call" | custom-call | tf_op jit(solution)/shard_map/second_scatter/pallas_call | solution.py:396
  1958.6 34.4 %orthogonalise.10 = (f32[8,512,512]{2,1,0:T(8,128)}, f32[8,128]{1,0:T(8,128)}, f32[8,128]{1,0:T(8,128)}, f32[8,128]{1,0:T(8,128)}) custom-call(f32[8,512,512]{2,1,0:T(8,128)} %get-tuple-element.57.refs_0_, f32[8,512,512]{2,1,0:T(8,128)} %get-tuple-element.40.refs_1_, f32[8,512,512]{2,1,0:T(8,128)} %get-tuple-element.46.refs_2_, ...), custom_call_target="tpu_custom_call" | custom-call | tf_op jit(solution)/shard_map/orthogonalise/pallas_call | solution.py:549
  1993.0 1.2 slice.41
  1994.3 1.2 slice.36
  1995.5 247.2 %gather_first.9 = (bf16[8,3,2048,384]{3,2,1,0:T(8,128)(2,1)}, f32[8,512,512]{2,1,0:T(8,128)}, f32[8,512,512]{2,1,0:T(8,128)}, f32[8,512,512]{2,1,0:T(8,128)}, f32[8,512,512]{2,1,0:T(8,128)}) custom-call(f32[8,512,512]{2,1,0:T(8,128)} %get-tuple-element.60.u, f32[8,128]{1,0:T(8,128)} %get-tuple-element.61.inv, f32[144]{0:T(256)} %reshape.36.w, ...), custom_call_target="tpu_custom_call" | custom-call | tf_op jit(solution)/shard_map/gather_first/pallas_call | solution.py:228
  2242.8 194.9 %second_scatter.9 = (f32[8,512,512]{2,1,0:T(8,128)}, f32[16,256,512]{2,1,0:T(8,128)}, f32[16,256,512]{2,1,0:T(8,128)}) custom-call(bf16[8,3,2048,384]{3,2,1,0:T(8,128)(2,1)} %get-tuple-element.62.t2, bf16[3,3072,2048]{2,1,0:T(8,128)(2,1)} %shard_map.68.rs), custom_call_target="tpu_custom_call" | custom-call | tf_op jit(solution)/shard_map/second_scatter/pallas_call | solution.py:396
  2437.7 38.8 %orthogonalise.11 = (f32[8,512,512]{2,1,0:T(8,128)}, f32[8,128]{1,0:T(8,128)}, f32[8,128]{1,0:T(8,128)}, f32[8,128]{1,0:T(8,128)}) custom-call(f32[8,512,512]{2,1,0:T(8,128)} %get-tuple-element.63.refs_0_, f32[8,512,512]{2,1,0:T(8,128)} %get-tuple-element.40.refs_1_, f32[8,512,512]{2,1,0:T(8,128)} %get-tuple-element.46.refs_2_, ...), custom_call_target="tpu_custom_call" | custom-call | tf_op jit(solution)/shard_map/orthogonalise/pallas_call | solution.py:549
  2476.5 1.2 slice.43
  2477.7 1.2 slice.42
  2478.9 1.2 slice.37
  2480.1 3.8 stack.6
  2483.9 3.7 stack.7
  2487.6 9.2 multiply_multiply_fusion
  2496.8 9.9 mul.28
  2506.7 11.5 copy.13
  2518.2 10.8 mul.30
